TPU v7x, 32 devices: a whole 2x2x4 slice. The times are simulated.
32 devices in a mesh: ctx: 8 (over z, x), head: 4 (over y, core).
Axes of the slice: x: 2, y: 2, z: 4, core: 2. Of those that a mesh axis runs over, the one named last changes fastest.
Arguments:
- queries: bfloat16 [2048, 32, 128], P('ctx', 'head'), may hold values from -20 to 20
- key_states: bfloat16 [2048, 4, 128], P('ctx', 'head'), may hold values from -20 to 20
- segment_ids: int32 [2048], P('ctx'), may hold values from 0 to 5, never falling along the last dimension, each value on 1 to 1280 neighbouring positions
Outputs:
- row_entropy: float32 [32, 2048], P('head', 'ctx')
- row_max: float32 [32, 2048], P('head', 'ctx')
- token_entropy: float32 [2048], P('ctx')
- head_entropy: float32 [32], P('head')
- head_peak: float32 [32], P('head')
Inputs may be any that keep to these rules, and one draw needn't show every extreme that they name: `segment_ids`: segment numbers never fall along the sequence; a document holds at most 1280 tokens.
All inputs are finite; a program needn't handle non-finite values.
Results may differ from a plain program's by a relative error of at most 0.0003.
Values may be sent and summed in bfloat16 or wider, within the bound.
A program may use at most 64 MiB of HBM per device.

v0:
```python
from functools import partial

import jax
import jax.numpy as jnp
from jax import lax
from jax.sharding import PartitionSpec as P

HEADS = 32


NEG_FILL = -1e30


def merged(part, axis, combine):
    gathered = jax.tree.map(lambda a: lax.all_gather(a, axis), part)

    def take(source):
        return jax.tree.map(lambda a: lax.dynamic_index_in_dim(a, source, 0, False), gathered)

    return lax.fori_loop(
        1, lax.axis_size(axis), lambda source, state: combine(state, take(source)), take(0)
    )


def keep_same(state):
    return state


def combine_totals(first, second):
    return (first[0] + second[0], jnp.maximum(first[1], second[1]))


def shards(queries, key_states, segment_ids):
    tok_rows = queries.shape[0]
    heads_local = queries.shape[1]
    head_dim = queries.shape[2]
    kv_local = key_states.shape[1]
    per_kv = heads_local // kv_local
    score_scale = head_dim ** (-0.5)
    ctx_count = lax.axis_size("ctx")
    my_index = lax.axis_index("ctx")
    positions = my_index * tok_rows + jnp.arange(tok_rows, dtype=jnp.int32)
    group_count = 1
    q_groups = queries.transpose(1, 0, 2)[None]
    q_pos = positions[None]
    q_seg = segment_ids[None]
    far_pos = jnp.max(q_pos, axis=1)
    seg_high = jnp.max(q_seg, axis=1)
    seg_low = jnp.min(q_seg, axis=1)
    grouped = [q_groups[0].reshape(kv_local, per_kv * tok_rows, head_dim)]

    def update_group(group_id, key_block, seg_block, key_pos, state):
        peaks, totals, moments = state
        logits = (
            jnp.einsum(
                "krd,pkd->krp", grouped[group_id], key_block, preferred_element_type=jnp.float32
            )
            * score_scale
        )
        logits = logits.reshape(heads_local, tok_rows, key_block.shape[0])
        visible = (key_pos[None, :] <= q_pos[group_id][:, None]) & (
            seg_block[None, :] == q_seg[group_id][:, None]
        )
        visible = visible[None]
        new_peak = jnp.maximum(peaks, jnp.max(jnp.where(visible, logits, NEG_FILL), axis=2))
        factor = jnp.exp(peaks - new_peak)
        shifted = logits - new_peak[:, :, None]
        expo = jnp.where(visible, jnp.exp(shifted), 0.0)
        new_totals = totals * factor + jnp.sum(expo, axis=2)
        new_moments = factor * (moments + (peaks - new_peak) * totals) + jnp.sum(
            expo * shifted, axis=2
        )
        return (new_peak, new_totals, new_moments)

    start_state = (
        jnp.full((group_count, heads_local, tok_rows), NEG_FILL, jnp.float32),
        jnp.zeros((group_count, heads_local, tok_rows), jnp.float32),
        jnp.zeros((group_count, heads_local, tok_rows), jnp.float32),
    )
    key_piece = lax.all_gather(key_states, "ctx", axis=0, tiled=True)
    seg_piece = lax.all_gather(segment_ids, "ctx", axis=0, tiled=True)
    span = key_piece.shape[0]
    width = 512

    def one_block(block_number, state):
        begin = block_number * width
        key_block = lax.dynamic_slice_in_dim(key_piece, begin, width, 0)
        seg_block = lax.dynamic_slice_in_dim(seg_piece, begin, width, 0)
        key_pos = begin + jnp.arange(width, dtype=jnp.int32)
        peaks, totals, moments = state
        is_live = (
            (far_pos[0] >= begin)
            & (seg_high[0] >= jnp.min(seg_block))
            & (seg_low[0] <= jnp.max(seg_block))
        )
        result = lax.cond(
            is_live,
            partial(update_group, 0, key_block, seg_block, key_pos),
            keep_same,
            (peaks[0], totals[0], moments[0]),
        )
        out_peaks = [result[0]]
        out_totals = [result[1]]
        out_moments = [result[2]]
        return (jnp.stack(out_peaks), jnp.stack(out_totals), jnp.stack(out_moments))

    peaks, totals, moments = lax.fori_loop(0, span // width, one_block, start_state)
    entropy = jnp.log(totals) - moments / totals
    row_entropy = entropy[0]
    row_max = peaks[0]
    token_entropy = lax.psum(jnp.sum(row_entropy, axis=0), "head") / HEADS
    local_sums = jnp.sum(row_entropy, axis=1)
    local_peaks = jnp.max(row_max, axis=1)
    entropy_sums, head_peak = merged((local_sums, local_peaks), "ctx", combine_totals)
    head_entropy = entropy_sums / (tok_rows * ctx_count)
    return (row_entropy, row_max, token_entropy, head_entropy, head_peak)


def solution(mesh):
    return jax.shard_map(
        shards,
        mesh=mesh,
        in_specs=(P("ctx", "head", None), P("ctx", "head", None), P("ctx")),
        out_specs=(P("head", "ctx"), P("head", "ctx"), P("ctx"), P("head"), P("head")),
        check_vma=False,
    )
```

profile of v0, /device:TPU:0, one launch (start us, length us, event | category | flops | bytes accessed | tf_op | source)
XLA Modules:
  0.0 130.1 jit_solution(18256471266170846318)
XLA Ops:
  0.6 0.6 add_reduce_fusion
  1.3 1.3 %fusion.11 = (s32[]{:T(128)}, s32[]{:T(128)}) fusion(s32[256]{0:T(256)} %param.11), kind=kLoop, calls=%fused_computation.27 | loop fusion | flops 510 | bytes 1032 | tf_op jit(solution)/shard_map/reduce_min | solution.py:49
  2.6 33.2 %all_gather.19 = bf16[2048,1,128]{2,0,1:T(8,128)(2,1)S(1)} all-gather(bf16[256,1,128]{2,0,1:T(8,128)(2,1)} %param.10), channel_id=1, replica_groups=mesh['ctx'=8,'head'=4] {'ctx'}, dimensions={0}, use_global_device_ids=true | all-gather | bytes 589824 | tf_op jit(solution)/shard_map/all_gather | solution.py:80
  35.8 1.1 copy.11
  36.9 20.9 %all-gather.2 = s32[8,1,256]{2,1,0:T(1,128)S(1)} all-gather(s32[1,1,256]{2,1,0:T(1,128)} %bitcast.87), channel_id=1, replica_groups=mesh['ctx'=8,'head'=4] {'ctx'}, dimensions={0}, use_global_device_ids=true | all-gather | bytes 9216 | tf_op jit(solution)/shard_map/all_gather | solution.py:81
  57.8 24.6 %while.36 = (s32[]{:T(128)}, f32[1,8,256]{2,1,0:T(8,128)S(1)}, f32[1,8,256]{2,1,0:T(8,128)S(1)}, f32[1,8,256]{2,1,0:T(8,128)S(1)}, s32[1]{0:T(128)}, /*index=5*/...) while((s32[]{:T(128)}, f32[1,8,256]{2,1,0:T(8,128)S(1)}, ...), condition=%wide.region_11.12_spmd.clone, body=%wide.region_3.11_spmd.clone.sunk | while | flops 278279936 | bytes 14765457 | solution.py:107
  57.9 0.8 fusion.13
  61.9 8.4 %conditional.3 = (f32[1,8,256]{2,1,0:T(8,128)S(1)}, f32[1,8,256]{2,1,0:T(8,128)S(1)}, f32[1,8,256]{2,1,0:T(8,128)S(1)}) conditional(s32[]{:T(128)} %convert_element_type.9, (f32[8,256]{1,0:T(8,128)S(1)}, f32[8,256]{1,0:T(8,128)S(1)}, f32[8,256]{1,0:T(8,128)S(1)}) %tuple.117, (s32[]{:T(128)}, s32[512]{0:T(512)S(1)}, s32[]{:T(128)}, s32[512]{0:T(512)S(1)}, ...), branch_computations={%region_6.0_spmd, %region_7.10_spmd} | conditional | flops 278278912 | bytes 14757924 | solution.py:96
  61.9 0.9 compare_and_fusion
  62.8 0.5 broadcast_in_dim.24
  63.3 0.6 copy.12
  63.9 2.7 %fusion.2 = (f32[2048]{0:T(1024)S(1)}, f32[512,2048]{1,0:T(8,128)}) fusion(pred[2048,512]{0,1:T(8,128)(4,1)S(1)} %bitcast.71, bf16[1,2048,128]{2,1,0:T(8,128)(2,1)S(1)} %get-tuple-element.381, bf16[2048,1,128]{2,0,1:T(8,128)(2,1)S(1)} %get-tuple-element.379, s32[]{:T(128)} %get-tuple-element.380), kind=kOutput, calls=%fused_computation.3 | convolution fusion | flops 271579136 | bytes 5906436 | tf_op jit(solution)/shard_map/while/body/eval_jaxpr/cond/branch_1_fun/krd,pkd->krp/dot_general | solution.py:55
  66.7 3.6 %multiply_reduce_fusion = (f32[2048]{0:T(1024)S(1)}, f32[2048]{0:T(1024)S(1)}) fusion(pred[2048,512]{0,1:T(8,128)(4,1)S(1)} %bitcast.72, f32[512,2048]{1,0:T(8,128)} %get-tuple-element.504, f32[2048]{0:T(1024)S(1)} %bitcast.78), kind=kLoop, calls=%fused_computation.4 | loop fusion | flops 6287360 | bytes 5267456 | tf_op jit(solution)/shard_map/while/body/eval_jaxpr/cond/branch_1_fun/reduce_sum | solution.py:70
  70.3 0.8 fusion.13
  74.4 0.8 fusion.13
  78.4 0.8 fusion.13
  82.4 0.0 copy-start
  82.4 0.7 fusion.10
  83.2 0.0 copy-done.2
  83.2 0.6 dynamic-slice
  84.4 0.2 dynamic-update-slice
  84.7 0.1 reduce_max.59
  84.8 0.2 dynamic-update-slice.1
  85.0 37.9 %all-reduce.2 = (f32[64]{0:T(128)S(1)}, f32[64]{0:T(128)S(1)}) all-reduce(f32[64]{0:T(128)S(1)} %dynamic-update-slice, f32[64]{0:T(128)S(1)} %dynamic-update-slice.1), channel_id=2, replica_groups=mesh['ctx'=8,'head'=4] {'ctx'}, use_global_device_ids=true, to_apply=%add | all-reduce | flops 128 | bytes 1024
  122.9 0.1 reshape.112
  123.0 0.1 reshape.113
  123.1 0.3 while.35
  123.4 0.0 copy-start.1
  123.4 0.5 broadcast_multiply_fusion.1
  123.9 5.6 %psum.7 = f32[256]{0:T(256)S(1)} all-reduce(f32[256]{0:T(256)S(1)} %get-tuple-element.459), channel_id=1, replica_groups=mesh['ctx'=8,'head'=4] {'head'}, use_global_device_ids=true, to_apply=%region_13.14 | all-reduce | flops 256 | bytes 2048 | tf_op jit(solution)/shard_map/psum | solution.py:111
  129.5 0.6 broadcast_multiply_fusion
  130.1 0.0 copy-done.1
  (33 shorter events, 0.2 us)
Async XLA Ops:
  57.8 25.3 %copy-start.2 = (u32[32]{0:T(128)S(1)}, u32[32]{0:T(128)}, u32[]{:S(2)}) copy-start(u32[32]{0:T(128)} %constant.130) | copy-start | bytes 388
  82.4 47.7 %copy-start = (f32[1,8,256]{2,1,0:T(8,128)}, f32[1,8,256]{2,1,0:T(8,128)S(1)}, u32[]{:S(2)}) copy-start(f32[1,8,256]{2,1,0:T(8,128)S(1)} %get-tuple-element.418) | copy-start | bytes 24580
  123.4 6.7 %copy-start.1 = (f32[8]{0:T(128)}, f32[8]{0:T(128)S(1)}, u32[]{:S(2)}) copy-start(f32[8]{0:T(128)S(1)} %get-tuple-element.415) | copy-start | bytes 100
where the time goes:
time: 131 us; the launch traced here: 130 us
  blocking collectives  97.7 us (75%)
  loops' own time  13.2 us (10%)
  other arithmetic  11.6 us (9%)
  local copies, waits for them, and re-layouts  3.51 us (3%)
  matrix products  2.74 us (2%)
  between operations  1.35 us (1%)
    unnamed x1, blocking collectives  37.9 us
    all_gather x1, blocking collectives, shards(): key_piece = lax.all_gather(key_states, 'ctx', axis=0, tiled=True)  33.2 us
    all_gather x1, blocking collectives, shards(): seg_piece = lax.all_gather(segment_ids, 'ctx', axis=0, tiled=True)  20.9 us
    another operation x1, loops' own time, shards(): lax.fori_loop(0, span // width, one_block, start_state)  12.9 us
    psum x1, blocking collectives, shards(): token_entropy = lax.psum(jnp.sum(row_entropy, axis=0), 'head') / HEADS  5.63 us
    reduce_sum x1, other arithmetic, update_group(): jnp.sum(expo * shifted, axis=2)  3.57 us
    reduce_max x4, other arithmetic, one_block(): jnp.max(seg_block)  3.15 us
    dot_general x1, matrix products, update_group(): jnp.einsum('krd,pkd->krp', grouped[group_id], key_block, preferred_elemen...  2.74 us

commit v1 on v0

v1 whole, which is shorter than its diff:
```python
from functools import partial

import jax
import jax.numpy as jnp
from jax import lax
from jax.experimental import pallas as pl
from jax.experimental.pallas import tpu as pltpu
from jax.sharding import PartitionSpec as P

HEADS = 32
MESH = pl.DeviceIdType.MESH
NEG = -1e30
LOG2E = 1.4426950408889634
LN2 = 0.6931471805599453


def kernel(
    ctx_n, head_n, reach, q_hbm, k_ref, seg_ref,
    ent_ref, max_ref, tok_ref, hent_ref, hpeak_ref,
    q_in, q_t, k_col, k_x, seg_col, seg_x, bias, peaks, totals, moments,
    tok_out, tok_in, stat_out, stat_in, q_sem, send_sem, recv_sem, tok_sem, stat_sem,
):
    rows, heads, dim = q_in.shape
    scale = dim ** (-0.5)
    to_log2 = scale * LOG2E
    c = lax.axis_index("ctx")
    h_me = lax.axis_index("head")
    groups = ctx_n // 2
    steps = reach // 2
    g = c // 2
    m = c % 2

    q_copy = pltpu.make_async_copy(q_hbm, q_in, q_sem)
    q_copy.start()

    barrier = pltpu.get_barrier_semaphore()
    for o in range(1, ctx_n):
        pl.semaphore_signal(barrier, 1, device_id={"ctx": lax.rem(c + o, ctx_n)}, device_id_type=MESH)
    for o in range(1, head_n):
        pl.semaphore_signal(barrier, 1, device_id={"head": lax.rem(h_me + o, head_n)}, device_id_type=MESH)
    pl.semaphore_wait(barrier, ctx_n + head_n - 2)

    def send(lane, slot, src, dst, target):
        keys = pltpu.make_async_remote_copy(
            src[0], dst[0], send_sem.at[lane, slot, 0], recv_sem.at[lane, slot, 0],
            device_id={"ctx": target}, device_id_type=MESH)
        segs = pltpu.make_async_remote_copy(
            src[1], dst[1], send_sem.at[lane, slot, 1], recv_sem.at[lane, slot, 1],
            device_id={"ctx": target}, device_id_type=MESH)
        return keys, segs

    own = (k_ref, seg_ref)

    def col(s):
        return (k_col.at[s], seg_col.at[s])

    def across(s):
        return (k_x.at[s], seg_x.at[s])

    def column_send(s):
        return send(0, s, own, col(s), jnp.minimum(g + s, groups - 1) * 2 + m)

    def own_across():
        return send(1, 0, own, across(0), c + 1 - 2 * m)

    def relay(s):
        return send(1, s, col(s), across(s), c + 1 - 2 * m)

    far = steps + 1

    def far_send():
        return send(1, far, own, across(far), jnp.minimum(g + far, groups - 1) * 2)

    def go(copies):
        for copy in copies:
            copy.start()

    def sent(copies):
        for copy in copies:
            copy.wait_send()

    def came(copies):
        for copy in copies:
            copy.wait_recv()

    def column_ok(s):
        return g + s < groups

    def relay_ok(s):
        return (s <= g) & ((m == 1) | (2 * s + 1 <= reach))

    def from_partner_ok(s):
        return (s <= g) & ((m == 0) | (2 * s + 1 <= reach))

    odd = reach % 2 == 1
    far_ok = (m == 1) & (g + far < groups)
    from_far_ok = (m == 0) & (far <= g)

    @pl.when(m == 0)
    def _():
        go(own_across())

    for s in range(1, steps + 1):
        @pl.when(column_ok(s))
        def _():
            go(column_send(s))
    if odd:
        @pl.when(far_ok)
        def _():
            go(far_send())

    q_copy.wait()
    q_t[...] = jnp.swapaxes(q_in[...].astype(jnp.float32), 0, 1).astype(jnp.bfloat16)

    seg_row = seg_ref[...]
    seg_cols = jnp.broadcast_to(seg_row.astype(jnp.float32), (128, rows)).T
    key_at = lax.broadcasted_iota(jnp.int32, (rows, rows), 0)
    row_at = lax.broadcasted_iota(jnp.int32, (rows, rows), 1)
    same = seg_cols[:, :1] == seg_row.astype(jnp.float32)
    bias[...] = jnp.where(same & (key_at <= row_at), 0.0, NEG)

    def block_of(keys, head):
        raw = lax.dot_general(
            keys[...], q_t[head], (((1,), (1,)), ((), ())), preferred_element_type=jnp.float32)
        raw = raw + bias[...]
        peak = jnp.max(raw, axis=0, keepdims=True)
        shifted = (raw - peak) * to_log2
        expo = jnp.exp2(shifted)
        return (peak, jnp.sum(expo, axis=0, keepdims=True),
                jnp.sum(expo * shifted, axis=0, keepdims=True))

    for head in range(heads):
        peak, total, moment = block_of(k_ref, head)
        at = pl.ds(head, 1)
        peaks[at, :] = peak
        totals[at, :] = total
        moments[at, :] = moment

    first_seg = seg_row[:, :1]

    def add_block(keys, segs):
        hidden = rows - jnp.sum((segs[...] == first_seg).astype(jnp.int32), axis=1, keepdims=True)
        at_key = lax.broadcasted_iota(jnp.int32, (rows, rows), 0)
        bias[...] = jnp.where((at_key >= hidden) & (seg_row == first_seg), 0.0, NEG)
        for head in range(heads):
            peak, total, moment = block_of(keys, head)
            at = pl.ds(head, 1)
            old = peaks[at, :]
            top = jnp.maximum(old, peak)
            down = (old - top) * to_log2
            fresh = (peak - top) * to_log2
            keep = jnp.exp2(down)
            take = jnp.exp2(fresh)
            held = totals[at, :]
            peaks[at, :] = top
            moments[at, :] = keep * (moments[at, :] + down * held) + take * (moment + fresh * total)
            totals[at, :] = held * keep + total * take

    @pl.loop(1, steps + 1)
    def _(s):
        @pl.when(s <= g)
        def _():
            came(column_send(s))

            @pl.when(relay_ok(s))
            def _():
                go(relay(s))

            add_block(k_col.at[s], seg_col.at[s])

    @pl.loop(0, far + 1 if odd else far)
    def _(s):
        near = (s <= steps) & from_partner_ok(s) & ((m == 1) | (s >= 1))
        distant = (s == far) & from_far_ok

        @pl.when(near | distant)
        def _():
            came(relay(s))
            add_block(k_x.at[s], seg_x.at[s])

    entropy = jnp.log(totals[...]) - moments[...] * LN2 / totals[...]
    tops = peaks[...] * scale
    tok_part = jnp.sum(entropy, axis=0, keepdims=True)
    diag = (lax.broadcasted_iota(jnp.int32, (heads, 128), 0)
            == lax.broadcasted_iota(jnp.int32, (heads, 128), 1))
    sums = jnp.sum(jnp.where(diag, jnp.sum(entropy, axis=1, keepdims=True), 0.0), axis=0, keepdims=True)
    highs = jnp.max(jnp.where(diag, jnp.max(tops, axis=1, keepdims=True), NEG), axis=0, keepdims=True)
    stat_out[0:1, :] = sums
    stat_out[1:2, :] = highs
    tok_out[...] = tok_part
    ent_ref[...] = entropy
    max_ref[...] = tops

    def stat_send(o):
        return pltpu.make_async_remote_copy(
            stat_out, stat_in.at[o], stat_sem.at[0, o], stat_sem.at[1, o],
            device_id={"ctx": lax.rem(c + o, ctx_n)}, device_id_type=MESH)

    def tok_send(o):
        return pltpu.make_async_remote_copy(
            tok_out, tok_in.at[o], tok_sem.at[0, o], tok_sem.at[1, o],
            device_id={"head": lax.rem(h_me + o, head_n)}, device_id_type=MESH)

    for o in range(1, ctx_n):
        stat_send(o).start()
    for o in range(1, head_n):
        tok_send(o).start()

    @pl.when(m == 0)
    def _():
        sent(own_across())

    for s in range(1, steps + 1):
        @pl.when(column_ok(s))
        def _():
            sent(column_send(s))

        @pl.when(relay_ok(s))
        def _():
            sent(relay(s))
    if odd:
        @pl.when(far_ok)
        def _():
            sent(far_send())

    for o in range(1, head_n):
        tok_send(o).wait()
        tok_part = tok_part + tok_in[o]
    tok_ref[...] = tok_part / HEADS
    for o in range(1, ctx_n):
        stat_send(o).wait()
        sums = sums + stat_in[o, 0:1, :]
        highs = jnp.maximum(highs, stat_in[o, 1:2, :])
    hent_ref[...] = (sums / (rows * ctx_n))[:, :heads]
    hpeak_ref[...] = highs[:, :heads]


def shards(ctx_n, head_n, queries, key_states, segment_ids):
    rows, heads, dim = queries.shape
    longest = rows * ctx_n * 5 // 8
    reach = min(ctx_n - 1, (longest - 1 + rows - 1) // rows)
    slots = reach // 2 + 2
    vmem = pl.BlockSpec(memory_space=pltpu.VMEM)
    f32 = jnp.float32
    dma = pltpu.SemaphoreType.DMA
    ent, top, tok, hent, hpeak = pl.pallas_call(
        partial(kernel, ctx_n, head_n, reach),
        out_shape=[
            jax.ShapeDtypeStruct((heads, rows), f32),
            jax.ShapeDtypeStruct((heads, rows), f32),
            jax.ShapeDtypeStruct((1, rows), f32),
            jax.ShapeDtypeStruct((1, heads), f32),
            jax.ShapeDtypeStruct((1, heads), f32),
        ],
        in_specs=[pl.BlockSpec(memory_space=pl.ANY), vmem, vmem],
        out_specs=[vmem] * 5,
        scratch_shapes=[
            pltpu.VMEM((rows, heads, dim), jnp.bfloat16),
            pltpu.VMEM((heads, rows, dim), jnp.bfloat16),
            pltpu.VMEM((slots, rows, dim), jnp.bfloat16),
            pltpu.VMEM((slots, rows, dim), jnp.bfloat16),
            pltpu.VMEM((slots, 1, rows), jnp.int32),
            pltpu.VMEM((slots, 1, rows), jnp.int32),
            pltpu.VMEM((rows, rows), f32),
            pltpu.VMEM((heads, rows), f32),
            pltpu.VMEM((heads, rows), f32),
            pltpu.VMEM((heads, rows), f32),
            pltpu.VMEM((1, rows), f32),
            pltpu.VMEM((head_n, 1, rows), f32),
            pltpu.VMEM((2, 128), f32),
            pltpu.VMEM((ctx_n, 2, 128), f32),
            dma(()),
            dma((2, slots, 2)),
            dma((2, slots, 2)),
            dma((2, head_n)),
            dma((2, ctx_n)),
        ],
        compiler_params=pltpu.CompilerParams(collective_id=0, has_side_effects=True),
    )(queries, key_states.reshape(rows, dim), segment_ids.reshape(1, rows))
    return (ent, top, tok.reshape(rows), hent.reshape(heads), hpeak.reshape(heads))


def solution(mesh):
    return jax.shard_map(
        partial(shards, mesh.shape["ctx"], mesh.shape["head"]),
        mesh=mesh,
        in_specs=(P("ctx", "head", None), P("ctx", "head", None), P("ctx")),
        out_specs=(P("head", "ctx"), P("head", "ctx"), P("ctx"), P("head"), P("head")),
        check_vma=False,
    )
```

time: 131 us -> 28.4 us (0.22)
  blocking collectives: 97.7 us -> 0 us
  Pallas kernels: 0 us -> 23.6 us
  loops' own time: 13.2 us -> 0 us
  other arithmetic: 11.6 us -> 0 us
  matrix products: 2.74 us -> 0 us
    all_gather x2 -> x0, blocking collectives: 54.1 us -> none  [the longest x1 33.2 us: shards(): key_piece = lax.all_gather(key_states, 'ctx', axis=0, tiled=True)]
    unnamed x1 -> x0, blocking collectives: 37.9 us -> none
    pallas_call x0 -> x1, Pallas kernels: none -> 23.6 us  [shards(): pl.pallas_call(partial(kernel, ctx_n, head_n, reach), out_shape=[jax.Shap...]
    another operation x6 -> x0, loops' own time: 13.2 us -> none  [the longest x1 12.9 us: shards(): lax.fori_loop(0, span // width, one_block, start_state)]
    psum x1 -> x0, blocking collectives: 5.63 us -> none  [shards(): token_entropy = lax.psum(jnp.sum(row_entropy, axis=0), 'head') / HEADS]
    reduce_sum x2 -> x0, other arithmetic: 4.3 us -> none  [the longest x1 3.57 us: update_group(): jnp.sum(expo * shifted, axis=2)]
    reduce_max x6 -> x0, other arithmetic: 3.9 us -> none  [the longest x4 3.15 us: one_block(): jnp.max(seg_block)]
    unnamed x11 -> x15, local copies, waits for them, and re-layouts: 1.09 us -> 3.88 us
where the time goes in v1:
time: 28.4 us; the launch traced here: 28.1 us
  Pallas kernels  23.6 us (83%)
  local copies, waits for them, and re-layouts  3.88 us (14%)
  between operations  0.65 us (2%)
    pallas_call x1, Pallas kernels, shards(): pl.pallas_call(partial(kernel, ctx_n, head_n, reach), out_shape=[jax.Shap...  23.6 us
    unnamed x15, local copies, waits for them, and re-layouts  3.88 us

profile of v1, /device:TPU:0, one launch (start us, length us, event | category | flops | bytes accessed | tf_op | source)
XLA Modules:
  0.0 28.1 jit_solution(14764129330450746335)
XLA Ops:
  0.6 23.6 %shard_map.74 = (f32[8,256]{1,0:T(8,128)}, f32[8,256]{1,0:T(8,128)}, f32[1,256]{1,0:T(1,128)}, f32[1,8]{1,0:T(1,128)}, f32[1,8]{1,0:T(1,128)}) custom-call(bf16[256,8,128]{2,1,0:T(8,128)(2,1)} %q_hbm.1, bf16[256,128]{1,0:T(8,128)(2,1)} %bitcast.5, s32[1,256]{1,0:T(1,128)} %bitcast.6), custom_call_target="tpu_custom_call" | custom-call | tf_op jit(solution)/shard_map/pallas_call | solution.py:246
  24.2 0.0 copy-start.1
  24.2 0.7 %copy-done.1 = f32[8,256]{1,0:T(8,128)S(1)} copy-done((f32[8,256]{1,0:T(8,128)S(1)}, f32[8,256]{1,0:T(8,128)}, u32[]{:S(2)}) %copy-start.1) | copy-done | bytes 8216
  24.9 0.0 copy-start
  24.9 0.6 %copy.13 = f32[8,256]{1,0:T(8,128)} copy(f32[8,256]{1,0:T(8,128)S(1)} %copy-done.1) | data formatting | bytes 16384
  25.5 0.1 copy-done
  25.6 0.0 copy-start.2
  25.6 0.6 %copy.14 = f32[8,256]{1,0:T(8,128)} copy(f32[8,256]{1,0:T(8,128)S(1)} %copy-done) | data formatting | bytes 16384
  26.2 0.1 copy-done.2
  26.3 0.0 copy-start.4
  26.3 0.6 %copy.15 = f32[256]{0:T(256)} copy(f32[256]{0:T(256)S(1)} %bitcast.7) | data formatting | bytes 2048
  26.9 0.1 copy-done.4
  27.0 0.0 copy-start.3
  27.0 0.5 %copy.16 = f32[8]{0:T(128)} copy(f32[8]{0:T(128)S(1)} %bitcast.9) | data formatting | bytes 64
  27.5 0.1 copy-done.3
  27.6 0.5 %copy.17 = f32[8]{0:T(128)} copy(f32[8]{0:T(128)S(1)} %bitcast.8) | data formatting | bytes 64
Async XLA Ops:
  24.2 0.7 %copy-start.1 = (f32[8,256]{1,0:T(8,128)S(1)}, f32[8,256]{1,0:T(8,128)}, u32[]{:S(2)}) copy-start(f32[8,256]{1,0:T(8,128)} %get-tuple-element.20) | copy-start | bytes 24580
  24.9 0.7 %copy-start = (f32[8,256]{1,0:T(8,128)S(1)}, f32[8,256]{1,0:T(8,128)}, u32[]{:S(2)}) copy-start(f32[8,256]{1,0:T(8,128)} %get-tuple-element.21) | copy-start | bytes 24580
  25.6 0.7 %copy-start.2 = (f32[1,256]{1,0:T(1,128)S(1)}, f32[1,256]{1,0:T(1,128)}, u32[]{:S(2)}) copy-start(f32[1,256]{1,0:T(1,128)} %get-tuple-element.12) | copy-start | bytes 3076
  26.3 0.7 %copy-start.4 = (f32[1,8]{1,0:T(1,128)S(1)}, f32[1,8]{1,0:T(1,128)}, u32[]{:S(2)}) copy-start(f32[1,8]{1,0:T(1,128)} %get-tuple-element.13) | copy-start | bytes 100
  27.0 0.7 %copy-start.3 = (f32[1,8]{1,0:T(1,128)S(1)}, f32[1,8]{1,0:T(1,128)}, u32[]{:S(2)}) copy-start(f32[1,8]{1,0:T(1,128)} %get-tuple-element.14) | copy-start | bytes 100

commit v2 on v1

--- a/solution.py
+++ b/solution.py
@@ -19,6 +19,7 @@
     ent_ref, max_ref, tok_ref, hent_ref, hpeak_ref,
     q_in, q_t, k_col, k_x, seg_col, seg_x, bias, peaks, totals, moments,
     tok_out, tok_in, stat_out, stat_in, q_sem, send_sem, recv_sem, tok_sem, stat_sem,
+    up_sem, down_sem, pair_sem, slant_sem,
 ):
     rows, heads, dim = q_in.shape
     scale = dim ** (-0.5)
@@ -26,28 +27,53 @@
     c = lax.axis_index("ctx")
     h_me = lax.axis_index("head")
     groups = ctx_n // 2
-    steps = reach // 2
     g = c // 2
     m = c % 2
 
     q_copy = pltpu.make_async_copy(q_hbm, q_in, q_sem)
     q_copy.start()
 
+    def ring(o):
+        return {"ctx": jnp.clip(c + o, 0, ctx_n - 1)}
+
+    partner = {"ctx": c + 1 - 2 * m}
+    has_next = g + 1 < groups
+    has_last = g > 0
+    steps = reach // 2
+    far = steps + 1
+    odd = reach % 2 == 1
+
+    def tell(sem, target):
+        pl.semaphore_signal(sem, 1, device_id=target, device_id_type=MESH)
+
     barrier = pltpu.get_barrier_semaphore()
-    for o in range(1, ctx_n):
-        pl.semaphore_signal(barrier, 1, device_id={"ctx": lax.rem(c + o, ctx_n)}, device_id_type=MESH)
+    tell(barrier, partner)
     for o in range(1, head_n):
-        pl.semaphore_signal(barrier, 1, device_id={"head": lax.rem(h_me + o, head_n)}, device_id_type=MESH)
-    pl.semaphore_wait(barrier, ctx_n + head_n - 2)
-
-    def send(lane, slot, src, dst, target):
-        keys = pltpu.make_async_remote_copy(
-            src[0], dst[0], send_sem.at[lane, slot, 0], recv_sem.at[lane, slot, 0],
-            device_id={"ctx": target}, device_id_type=MESH)
-        segs = pltpu.make_async_remote_copy(
-            src[1], dst[1], send_sem.at[lane, slot, 1], recv_sem.at[lane, slot, 1],
-            device_id={"ctx": target}, device_id_type=MESH)
-        return keys, segs
+        tell(barrier, {"head": lax.rem(h_me + o, head_n)})
+
+    @pl.when(has_next)
+    def _():
+        tell(barrier, ring(2))
+
+    @pl.when(has_last)
+    def _():
+        tell(barrier, ring(-2))
+
+    pl.semaphore_wait(barrier, head_n + has_next.astype(jnp.int32) + has_last.astype(jnp.int32))
+
+    def parts(lane, src_slot, dst_slot, src, dst, target):
+        half = rows // 2
+        pieces = (
+            (src[1], dst[1]),
+            (src[0].at[pl.ds(0, half), :], dst[0].at[pl.ds(0, half), :]),
+            (src[0].at[pl.ds(half, half), :], dst[0].at[pl.ds(half, half), :]),
+        )
+        return [
+            pltpu.make_async_remote_copy(
+                source, place, send_sem.at[lane, src_slot, i], recv_sem.at[lane, dst_slot, i],
+                device_id=target, device_id_type=MESH)
+            for i, (source, place) in enumerate(pieces)
+        ]
 
     own = (k_ref, seg_ref)
 
@@ -57,57 +83,66 @@
     def across(s):
         return (k_x.at[s], seg_x.at[s])
 
-    def column_send(s):
-        return send(0, s, own, col(s), jnp.minimum(g + s, groups - 1) * 2 + m)
-
-    def own_across():
-        return send(1, 0, own, across(0), c + 1 - 2 * m)
-
-    def relay(s):
-        return send(1, s, col(s), across(s), c + 1 - 2 * m)
-
-    far = steps + 1
-
-    def far_send():
-        return send(1, far, own, across(far), jnp.minimum(g + far, groups - 1) * 2)
-
-    def go(copies):
-        for copy in copies:
+    def onward(s, src):
+        return parts(0, s, s + 1, src, col(s + 1), ring(2))
+
+    def cross(s, src):
+        return parts(1, s, s, src, across(s), partner)
+
+    def slant():
+        return parts(1, far, far, col(steps), across(far), ring(1))
+
+    def onward_ok(s):
+        return has_next & (s <= g) & (s + 1 <= steps)
+
+    def cross_ok(s):
+        return (s <= g) & ((m == 1) | (2 * s + 1 <= reach)) & ((m == 0) | (s >= 1))
+
+    def from_cross_ok(s):
+        return (s <= g) & ((m == 0) | (2 * s + 1 <= reach)) & ((m == 1) | (s >= 1))
+
+    slant_ok = has_next & (m == 1) & (steps <= g)
+    from_slant_ok = (m == 0) & (far <= g)
+
+    @pl.when(onward_ok(0))
+    def _():
+        for copy in onward(0, own):
             copy.start()
 
-    def sent(copies):
-        for copy in copies:
-            copy.wait_send()
-
-    def came(copies):
-        for copy in copies:
-            copy.wait_recv()
-
-    def column_ok(s):
-        return g + s < groups
-
-    def relay_ok(s):
-        return (s <= g) & ((m == 1) | (2 * s + 1 <= reach))
-
-    def from_partner_ok(s):
-        return (s <= g) & ((m == 0) | (2 * s + 1 <= reach))
-
-    odd = reach % 2 == 1
-    far_ok = (m == 1) & (g + far < groups)
-    from_far_ok = (m == 0) & (far <= g)
-
-    @pl.when(m == 0)
-    def _():
-        go(own_across())
-
-    for s in range(1, steps + 1):
-        @pl.when(column_ok(s))
-        def _():
-            go(column_send(s))
+    @pl.when(cross_ok(0))
+    def _():
+        for copy in cross(0, own):
+            copy.start()
+
     if odd:
-        @pl.when(far_ok)
-        def _():
-            go(far_send())
+        @pl.when((m == 1) & has_last)
+        def _():
+            tell(slant_sem, ring(-2))
+
+    @pl.when(has_next & (g == 0))
+    def _():
+        tell(up_sem, ring(2))
+
+    @pl.when(has_last & jnp.logical_not(has_next))
+    def _():
+        tell(down_sem, ring(-2))
+
+    def pass_tokens(up_now, down_now):
+        @pl.when(has_last & up_now)
+        def _():
+            pl.semaphore_wait(up_sem, 1)
+
+            @pl.when(has_next)
+            def _():
+                tell(up_sem, ring(2))
+
+        @pl.when(has_next & down_now)
+        def _():
+            pl.semaphore_wait(down_sem, 1)
+
+            @pl.when(has_last)
+            def _():
+                tell(down_sem, ring(-2))
 
     q_copy.wait()
     q_t[...] = jnp.swapaxes(q_in[...].astype(jnp.float32), 0, 1).astype(jnp.bfloat16)
@@ -156,27 +191,51 @@
             moments[at, :] = keep * (moments[at, :] + down * held) + take * (moment + fresh * total)
             totals[at, :] = held * keep + total * take
 
+    if odd:
+        @pl.when((m == 1) & has_next)
+        def _():
+            pl.semaphore_wait(slant_sem, 1)
+
     @pl.loop(1, steps + 1)
     def _(s):
         @pl.when(s <= g)
         def _():
-            came(column_send(s))
-
-            @pl.when(relay_ok(s))
-            def _():
-                go(relay(s))
+            arriving = onward(s - 1, col(s - 1))
+            forward = onward(s, col(s))
+            sideways = cross(s, col(s))
+            slanted = slant() if odd else []
+            for i, copy in enumerate(arriving):
+                copy.wait_recv()
+
+                @pl.when(onward_ok(s))
+                def _():
+                    forward[i].start()
+
+                @pl.when(cross_ok(s))
+                def _():
+                    sideways[i].start()
+
+                if odd:
+                    @pl.when(slant_ok & (s == steps))
+                    def _():
+                        slanted[i].start()
 
             add_block(k_col.at[s], seg_col.at[s])
+
+        pass_tokens(g == s, groups - 1 - g == s)
+
+    pass_tokens(g > steps, groups - 1 - g > steps)
+    tell(pair_sem, partner)
 
     @pl.loop(0, far + 1 if odd else far)
     def _(s):
-        near = (s <= steps) & from_partner_ok(s) & ((m == 1) | (s >= 1))
-        distant = (s == far) & from_far_ok
-
-        @pl.when(near | distant)
-        def _():
-            came(relay(s))
+        @pl.when(((s <= steps) & from_cross_ok(s)) | ((s == far) & from_slant_ok))
+        def _():
+            for copy in cross(s, across(s)):
+                copy.wait_recv()
             add_block(k_x.at[s], seg_x.at[s])
+
+    pl.semaphore_wait(pair_sem, 1)
 
     entropy = jnp.log(totals[...]) - moments[...] * LN2 / totals[...]
     tops = peaks[...] * scale
@@ -206,22 +265,21 @@
     for o in range(1, head_n):
         tok_send(o).start()
 
-    @pl.when(m == 0)
-    def _():
-        sent(own_across())
-
-    for s in range(1, steps + 1):
-        @pl.when(column_ok(s))
-        def _():
-            sent(column_send(s))
-
-        @pl.when(relay_ok(s))
-        def _():
-            sent(relay(s))
+    for s in range(steps + 1):
+        @pl.when(onward_ok(s))
+        def _():
+            for copy in onward(s, own if s == 0 else col(s)):
+                copy.wait_send()
+
+        @pl.when(cross_ok(s))
+        def _():
+            for copy in cross(s, own if s == 0 else col(s)):
+                copy.wait_send()
     if odd:
-        @pl.when(far_ok)
-        def _():
-            sent(far_send())
+        @pl.when(slant_ok)
+        def _():
+            for copy in slant():
+                copy.wait_send()
 
     for o in range(1, head_n):
         tok_send(o).wait()
@@ -233,6 +291,12 @@
         highs = jnp.maximum(highs, stat_in[o, 1:2, :])
     hent_ref[...] = (sums / (rows * ctx_n))[:, :heads]
     hpeak_ref[...] = highs[:, :heads]
+
+
+def write_out(*refs):
+    half = len(refs) // 2
+    for source, target in zip(refs[:half], refs[half:]):
+        target[...] = source[...]
 
 
 def shards(ctx_n, head_n, queries, key_states, segment_ids):
@@ -270,13 +334,20 @@
             pltpu.VMEM((2, 128), f32),
             pltpu.VMEM((ctx_n, 2, 128), f32),
             dma(()),
-            dma((2, slots, 2)),
-            dma((2, slots, 2)),
+            dma((2, slots, 3)),
+            dma((2, slots, 3)),
             dma((2, head_n)),
             dma((2, ctx_n)),
-        ],
+        ] + [pltpu.SemaphoreType.REGULAR] * 4,
         compiler_params=pltpu.CompilerParams(collective_id=0, has_side_effects=True),
     )(queries, key_states.reshape(rows, dim), segment_ids.reshape(1, rows))
+    results = (ent, top, tok, hent, hpeak)
+    ent, top, tok, hent, hpeak = pl.pallas_call(
+        write_out,
+        out_shape=[jax.ShapeDtypeStruct(a.shape, a.dtype) for a in results],
+        in_specs=[vmem] * 5,
+        out_specs=[vmem] * 5,
+    )(*results)
     return (ent, top, tok.reshape(rows), hent.reshape(heads), hpeak.reshape(heads))
 
 

time: 28.4 us -> 23.7 us (0.83)
  local copies, waits for them, and re-layouts: 3.88 us -> 0 us
  Pallas kernels: 23.6 us -> 22.9 us
    unnamed x15 -> x0, local copies, waits for them, and re-layouts: 3.88 us -> none
    pallas_call x1, Pallas kernels: 23.6 us -> 21.5 us  [shards(): pl.pallas_call(partial(kernel, ctx_n, head_n, reach), out_shape=[jax.Shap...]
    pallas_call x0 -> x1, Pallas kernels: none -> 1.34 us  [shards(): pl.pallas_call(write_out, out_shape=[jax.ShapeDtypeStruct(a.shape, a.dtyp...]
where the time goes in v2:
time: 23.7 us; the launch traced here: 23.5 us
  Pallas kernels  22.9 us (97%)
  between operations  0.64 us (3%)
    pallas_call x1, Pallas kernels, shards(): pl.pallas_call(partial(kernel, ctx_n, head_n, reach), out_shape=[jax.Shap...  21.5 us
    pallas_call x1, Pallas kernels, shards(): pl.pallas_call(write_out, out_shape=[jax.ShapeDtypeStruct(a.shape, a.dtyp...  1.34 us

profile of v2, /device:TPU:0, one launch (start us, length us, event | category | flops | bytes accessed | tf_op | source)
XLA Modules:
  0.0 23.5 jit_solution(12207978945408017755)
XLA Ops:
  0.6 21.5 %shard_map.74 = (f32[8,256]{1,0:T(8,128)}, f32[8,256]{1,0:T(8,128)}, f32[1,256]{1,0:T(1,128)}, f32[1,8]{1,0:T(1,128)}, f32[1,8]{1,0:T(1,128)}) custom-call(bf16[256,8,128]{2,1,0:T(8,128)(2,1)} %q_hbm.1, bf16[256,128]{1,0:T(8,128)(2,1)} %bitcast.5, s32[1,256]{1,0:T(1,128)} %bitcast.6), custom_call_target="tpu_custom_call" | custom-call | tf_op jit(solution)/shard_map/pallas_call | solution.py:310
  22.2 1.3 %shard_map.75 = (f32[8,256]{1,0:T(8,128)}, f32[8,256]{1,0:T(8,128)}, f32[1,256]{1,0:T(1,128)}, f32[1,8]{1,0:T(1,128)}, f32[1,8]{1,0:T(1,128)}) custom-call(f32[8,256]{1,0:T(8,128)} %get-tuple-element.15.refs_0_, f32[8,256]{1,0:T(8,128)} %get-tuple-element.16.refs_1_, f32[1,256]{1,0:T(1,128)} %get-tuple-element.17.refs_2_, f32[1,8]{1,0:T(1,128)} %get-tuple-element.18.refs_3_, ...), custom_call_target="tpu_custom_call" | custom-call | tf_op jit(solution)/shard_map/pallas_call | solution.py:345

commit v3 on v2

--- a/solution.py
+++ b/solution.py
@@ -15,10 +15,10 @@
 
 
 def kernel(
-    ctx_n, head_n, reach, q_hbm, k_ref, seg_ref,
+    ctx_n, head_n, reach, q_hbm, k_hbm, seg_hbm,
     ent_ref, max_ref, tok_ref, hent_ref, hpeak_ref,
-    q_in, q_t, k_col, k_x, seg_col, seg_x, bias, peaks, totals, moments,
-    tok_out, tok_in, stat_out, stat_in, q_sem, send_sem, recv_sem, tok_sem, stat_sem,
+    k_ref, seg_ref, q_in, q_t, k_col, k_x, seg_col, seg_x, bias, peaks, totals, moments,
+    tok_out, tok_in, stat_out, stat_in, q_sem, send_sem, recv_sem, tok_sem, stat_sem, k_sem,
     up_sem, down_sem, pair_sem, slant_sem,
 ):
     rows, heads, dim = q_in.shape
@@ -31,6 +31,10 @@
     m = c % 2
 
     q_copy = pltpu.make_async_copy(q_hbm, q_in, q_sem)
+    key_copy = pltpu.make_async_copy(k_hbm, k_ref, k_sem.at[0])
+    seg_copy = pltpu.make_async_copy(seg_hbm, seg_ref, k_sem.at[1])
+    key_copy.start()
+    seg_copy.start()
     q_copy.start()
 
     def ring(o):
@@ -60,6 +64,9 @@
         tell(barrier, ring(-2))
 
     pl.semaphore_wait(barrier, head_n + has_next.astype(jnp.int32) + has_last.astype(jnp.int32))
+
+    key_copy.wait()
+    seg_copy.wait()
 
     def parts(lane, src_slot, dst_slot, src, dst, target):
         half = rows // 2
@@ -310,15 +317,17 @@
     ent, top, tok, hent, hpeak = pl.pallas_call(
         partial(kernel, ctx_n, head_n, reach),
         out_shape=[
-            jax.ShapeDtypeStruct((heads, rows), f32),
-            jax.ShapeDtypeStruct((heads, rows), f32),
-            jax.ShapeDtypeStruct((1, rows), f32),
-            jax.ShapeDtypeStruct((1, heads), f32),
-            jax.ShapeDtypeStruct((1, heads), f32),
+            pltpu.VMEM((heads, rows), f32),
+            pltpu.VMEM((heads, rows), f32),
+            pltpu.VMEM((1, rows), f32),
+            pltpu.VMEM((1, heads), f32),
+            pltpu.VMEM((1, heads), f32),
         ],
-        in_specs=[pl.BlockSpec(memory_space=pl.ANY), vmem, vmem],
+        in_specs=[pl.BlockSpec(memory_space=pl.ANY)] * 3,
         out_specs=[vmem] * 5,
         scratch_shapes=[
+            pltpu.VMEM((rows, dim), jnp.bfloat16),
+            pltpu.VMEM((1, rows), jnp.int32),
             pltpu.VMEM((rows, heads, dim), jnp.bfloat16),
             pltpu.VMEM((heads, rows, dim), jnp.bfloat16),
             pltpu.VMEM((slots, rows, dim), jnp.bfloat16),
@@ -338,10 +347,11 @@
             dma((2, slots, 3)),
             dma((2, head_n)),
             dma((2, ctx_n)),
+            dma((2,)),
         ] + [pltpu.SemaphoreType.REGULAR] * 4,
         compiler_params=pltpu.CompilerParams(collective_id=0, has_side_effects=True),
     )(queries, key_states.reshape(rows, dim), segment_ids.reshape(1, rows))
-    results = (ent, top, tok, hent, hpeak)
+    results = [pltpu.with_memory_space_constraint(a, pltpu.VMEM) for a in (ent, top, tok, hent, hpeak)]
     ent, top, tok, hent, hpeak = pl.pallas_call(
         write_out,
         out_shape=[jax.ShapeDtypeStruct(a.shape, a.dtype) for a in results],

time: 23.7 us -> 21.6 us (0.911)
  Pallas kernels: 22.9 us -> 20.8 us
    pallas_call x1, Pallas kernels: 21.5 us -> 20.2 us  [shards(): pl.pallas_call(partial(kernel, ctx_n, head_n, reach), out_shape=[pltpu.VM...]
    pallas_call x1, Pallas kernels: 1.34 us -> 0.62 us  [shards(): pl.pallas_call(write_out, out_shape=[jax.ShapeDtypeStruct(a.shape, a.dtyp...]
where the time goes in v3:
time: 21.6 us; the launch traced here: 21.4 us
  Pallas kernels  20.8 us (96%)
  between operations  0.64 us (3%)
    pallas_call x1, Pallas kernels, shards(): pl.pallas_call(partial(kernel, ctx_n, head_n, reach), out_shape=[pltpu.VM...  20.2 us
    pallas_call x1, Pallas kernels, shards(): pl.pallas_call(write_out, out_shape=[jax.ShapeDtypeStruct(a.shape, a.dtyp...  0.62 us

profile of v3, /device:TPU:0, one launch (start us, length us, event | category | flops | bytes accessed | tf_op | source)
XLA Modules:
  0.0 21.4 jit_solution(14592039670178935718)
XLA Ops:
  0.6 20.2 %shard_map.74 = (f32[8,256]{1,0:T(8,128)S(1)}, f32[8,256]{1,0:T(8,128)S(1)}, f32[1,256]{1,0:T(1,128)S(1)}, f32[1,8]{1,0:T(1,128)S(1)}, f32[1,8]{1,0:T(1,128)S(1)}) custom-call(bf16[256,8,128]{2,1,0:T(8,128)(2,1)} %q_hbm.1, bf16[256,128]{1,0:T(8,128)(2,1)} %bitcast.5, s32[1,256]{1,0:T(1,128)} %bitcast.6), custom_call_target="tpu_custom_call" | custom-call | tf_op jit(solution)/shard_map/pallas_call | solution.py:317
  20.8 0.6 %shard_map.75 = (f32[8,256]{1,0:T(8,128)}, f32[8,256]{1,0:T(8,128)}, f32[1,256]{1,0:T(1,128)}, f32[1,8]{1,0:T(1,128)}, f32[1,8]{1,0:T(1,128)}) custom-call(f32[8,256]{1,0:T(8,128)S(1)} %get-tuple-element.15.refs_0_, f32[8,256]{1,0:T(8,128)S(1)} %get-tuple-element.16.refs_1_, f32[1,256]{1,0:T(1,128)S(1)} %get-tuple-element.17.refs_2_, ...), custom_call_target="tpu_custom_call" | custom-call | tf_op jit(solution)/shard_map/pallas_call | solution.py:355

commit v4 on v3

--- a/solution.py
+++ b/solution.py
@@ -180,10 +180,12 @@
 
     first_seg = seg_row[:, :1]
 
-    def add_block(keys, segs):
+    def set_bias(segs):
         hidden = rows - jnp.sum((segs[...] == first_seg).astype(jnp.int32), axis=1, keepdims=True)
         at_key = lax.broadcasted_iota(jnp.int32, (rows, rows), 0)
         bias[...] = jnp.where((at_key >= hidden) & (seg_row == first_seg), 0.0, NEG)
+
+    def add_block(keys):
         for head in range(heads):
             peak, total, moment = block_of(keys, head)
             at = pl.ds(head, 1)
@@ -227,7 +229,8 @@
                     def _():
                         slanted[i].start()
 
-            add_block(k_col.at[s], seg_col.at[s])
+            set_bias(seg_col.at[s])
+            add_block(k_col.at[s])
 
         pass_tokens(g == s, groups - 1 - g == s)
 
@@ -238,9 +241,12 @@
     def _(s):
         @pl.when(((s <= steps) & from_cross_ok(s)) | ((s == far) & from_slant_ok))
         def _():
-            for copy in cross(s, across(s)):
+            segs, *halves = cross(s, across(s))
+            segs.wait_recv()
+            set_bias(seg_x.at[s])
+            for copy in halves:
                 copy.wait_recv()
-            add_block(k_x.at[s], seg_x.at[s])
+            add_block(k_x.at[s])
 
     pl.semaphore_wait(pair_sem, 1)
 

time: 21.6 us -> 21.7 us (level)
  no operation moved by 1% of the time
where the time goes in v4:
time: 21.7 us; the launch traced here: 21.6 us
  Pallas kernels  20.9 us (96%)
  between operations  0.64 us (3%)
    pallas_call x1, Pallas kernels, shards(): pl.pallas_call(partial(kernel, ctx_n, head_n, reach), out_shape=[pltpu.VM...  20.3 us
    pallas_call x1, Pallas kernels, shards(): pl.pallas_call(write_out, out_shape=[jax.ShapeDtypeStruct(a.shape, a.dtyp...  0.62 us

profile of v4, /device:TPU:0, one launch (start us, length us, event | category | flops | bytes accessed | tf_op | source)
XLA Modules:
  0.0 21.6 jit_solution(3809774507001438147)
XLA Ops:
  0.6 20.3 %shard_map.74 = (f32[8,256]{1,0:T(8,128)S(1)}, f32[8,256]{1,0:T(8,128)S(1)}, f32[1,256]{1,0:T(1,128)S(1)}, f32[1,8]{1,0:T(1,128)S(1)}, f32[1,8]{1,0:T(1,128)S(1)}) custom-call(bf16[256,8,128]{2,1,0:T(8,128)(2,1)} %q_hbm.1, bf16[256,128]{1,0:T(8,128)(2,1)} %bitcast.5, s32[1,256]{1,0:T(1,128)} %bitcast.6), custom_call_target="tpu_custom_call" | custom-call | tf_op jit(solution)/shard_map/pallas_call | solution.py:323
  20.9 0.6 %shard_map.75 = (f32[8,256]{1,0:T(8,128)}, f32[8,256]{1,0:T(8,128)}, f32[1,256]{1,0:T(1,128)}, f32[1,8]{1,0:T(1,128)}, f32[1,8]{1,0:T(1,128)}) custom-call(f32[8,256]{1,0:T(8,128)S(1)} %get-tuple-element.15.refs_0_, f32[8,256]{1,0:T(8,128)S(1)} %get-tuple-element.16.refs_1_, f32[1,256]{1,0:T(1,128)S(1)} %get-tuple-element.17.refs_2_, ...), custom_call_target="tpu_custom_call" | custom-call | tf_op jit(solution)/shard_map/pallas_call | solution.py:361
